TPU v7x, 8 devices: a whole 2x2x1 slice. The times are simulated.
8 devices in a mesh: dp: 2 (over z, y), tp: 4 (over x, core).
Axes of the slice: x: 2, y: 2, z: 1, core: 2. Of those that a mesh axis runs over, the one named last changes fastest.
Arguments:
- w_up: bfloat16 [2, 2560, 10240], P(None, None, 'tp')
- w_down: bfloat16 [2, 10240, 2560], P(None, 'tp')
- saved_x: bfloat16 [2, 2, 4096, 2560], P(None, 'dp')
- saved_h: bfloat16 [2, 2, 4096, 10240], P(None, 'dp', None, 'tp')
- grad_out: bfloat16 [2, 4096, 2560], P('dp')
Outputs:
- output 1: bfloat16 [2, 4096, 2560], P('dp')
- output 2: float32 [2, 2560, 10240], P(None, 'dp', 'tp')
- output 3: float32 [2, 10240, 2560], P(None, 'tp', 'dp')
All inputs are finite; a program needn't handle non-finite values.
Results may differ from a plain program's by a relative error of at most 0.014246.
Values are sent between devices in bfloat16 or wider.
A program may use at most 1 GiB of HBM per device.

v0:
```python
import jax
import jax.numpy as jnp
import math
from jax import lax
from jax.sharding import PartitionSpec as P, NamedSharding

GELU_SCALE = math.sqrt(2.0 / math.pi)
GELU_CUBIC = 0.044715


def gelu_and_slope(pre_act):
    tanh_val = jnp.tanh(GELU_SCALE * (pre_act + GELU_CUBIC * pre_act * pre_act * pre_act))
    act_val = 0.5 * pre_act * (1.0 + tanh_val)
    act_slope = 0.5 * (1.0 + tanh_val) + 0.5 * pre_act * (1.0 - tanh_val * tanh_val) * GELU_SCALE * (1.0 + 3.0 * GELU_CUBIC * pre_act * pre_act)
    return act_val, act_slope


def solution(mesh):
    def local_backward(w_up, w_down, saved_x, saved_h, grad_out):
        grad_cur = grad_out
        up_list = []
        down_list = []
        for layer_idx in reversed(range(w_up.shape[0])):
            act_val, act_slope = gelu_and_slope(saved_h[layer_idx].astype(jnp.float32))
            d_act = jnp.einsum("bsd,fd->bsf", grad_cur, w_down[layer_idx], preferred_element_type=jnp.float32)
            d_pre = (d_act * act_slope).astype(jnp.bfloat16)
            part_sum = jnp.einsum("bsf,df->bsd", d_pre, w_up[layer_idx], preferred_element_type=jnp.float32).astype(jnp.bfloat16)
            full_sum = lax.psum(part_sum, "tp")
            grad_next = (grad_cur.astype(jnp.float32) + full_sum.astype(jnp.float32)).astype(jnp.bfloat16)
            local_down = jnp.einsum("bsf,bsd->fd", act_val.astype(jnp.bfloat16), grad_cur, preferred_element_type=jnp.float32)
            local_up = jnp.einsum("bsd,bsf->df", saved_x[layer_idx], d_pre, preferred_element_type=jnp.float32)
            down_list.append(lax.psum_scatter(local_down, "dp", scatter_dimension=1, tiled=True))
            up_list.append(lax.psum_scatter(local_up, "dp", scatter_dimension=0, tiled=True))
            grad_cur = grad_next
        return grad_cur, jnp.stack(up_list[::-1]), jnp.stack(down_list[::-1])

    return jax.shard_map(
        local_backward,
        mesh=mesh,
        in_specs=(P(None, None, "tp"), P(None, "tp", None), P(None, "dp", None, None), P(None, "dp", None, "tp"), P("dp", None, None)),
        out_specs=(P("dp", None, None), P(None, "dp", "tp"), P(None, "tp", "dp")),
        check_vma=False,
    )
```

profile of v0, /device:TPU:0, one launch (start us, length us, event | category | flops | bytes accessed | tf_op | source)
XLA Modules:
  0.0 1902.0 jit_solution(12501704205254322465)
XLA Ops:
  8.0 0.0 all-reduce.3.cloned.1.call-start
  8.0 80.3 %fusion.21 = bf16[4096,2560]{1,0:T(8,128)(2,1)} fusion(bf16[1,4096,2560]{2,1,0:T(8,128)(2,1)} %param.9, bf16[2,1,4096,2560]{3,2,1,0:T(8,128)(2,1)} %param.8, bf16[2,2560,2560]{2,1,0:T(8,128)(2,1)} %param.6), kind=kOutput, calls=%fused_computation.33 | convolution fusion | flops 53896806400 | bytes 76021760 | tf_op jit(solution)/shard_map/bsd,fd->bsf/dot_general | solution.py:25
  88.3 63.0 %fusion.66 = bf16[1,4096,2560]{2,1,0:T(8,128)(2,1)} fusion(bf16[4096,2560]{1,0:T(8,128)(2,1)} %fusion.21, bf16[2,2560,2560]{2,1,0:T(8,128)(2,1)} %param.5), kind=kOutput, calls=%fused_computation.82 | convolution fusion | flops 53697576960 | bytes 55050240 | tf_op jit(solution)/shard_map/bsf,df->bsd/dot_general | solution.py:27
  151.4 0.0 all-reduce.5.cloned.1.call-start
  151.5 353.5 %all-reduce.3.cloned.1.call-done = bf16[1,4096,2560]{2,1,0:T(8,128)(2,1)} async-done(((bf16[1,4096,2560]{2,1,0:T(8,128)(2,1)}), bf16[1,4096,2560]{2,1,0:T(8,128)(2,1)}) %all-reduce.3.cloned.1.call-update) | async-done | bytes 20971536 | tf_op jit(solution)/shard_map/psum | solution.py:28
  504.9 83.4 %fusion.35 = bf16[4096,2560]{1,0:T(8,128)(2,1)} fusion(bf16[2,1,4096,2560]{3,2,1,0:T(8,128)(2,1)} %param.8, bf16[2,2560,2560]{2,1,0:T(8,128)(2,1)} %param.6, bf16[1,4096,2560]{2,1,0:T(8,128)(2,1)} %all-reduce.3.cloned.1.call-done, bf16[1,4096,2560]{2,1,0:T(8,128)(2,1)} %param.9), kind=kOutput, calls=%fused_computation.47 | convolution fusion | flops 53938749440 | bytes 96993280 | tf_op jit(solution)/shard_map/bsd,fd->bsf/dot_general | solution.py:25
  588.3 63.1 %fusion.67 = bf16[1,4096,2560]{2,1,0:T(8,128)(2,1)} fusion(bf16[4096,2560]{1,0:T(8,128)(2,1)} %fusion.35, bf16[2,2560,2560]{2,1,0:T(8,128)(2,1)} %param.5), kind=kOutput, calls=%fused_computation.83 | convolution fusion | flops 53697576960 | bytes 55050240 | tf_op jit(solution)/shard_map/bsf,df->bsd/dot_general | solution.py:27
  651.4 0.0 reduce-scatter.7.cloned.1.call-start
  651.5 66.7 %fusion.71 = f32[2560,2560]{0,1:T(8,128)} fusion(bf16[4096,2560]{1,0:T(8,128)(2,1)} %fusion.21, bf16[2,1,4096,2560]{3,2,1,0:T(8,128)(2,1)} %param.7), kind=kOutput, calls=%fused_computation.85 | convolution fusion | flops 53687091200 | bytes 68157440 | tf_op jit(solution)/shard_map/bsd,bsf->df/dot_general | solution.py:31
  718.2 0.0 reduce-scatter.7.cloned.1.call-update
  718.2 0.0 reduce-scatter.5.cloned.1.call-start
  718.3 66.4 %fusion.68 = f32[2560,2560]{0,1:T(8,128)} fusion(bf16[4096,2560]{1,0:T(8,128)(2,1)} %fusion.35, bf16[2,1,4096,2560]{3,2,1,0:T(8,128)(2,1)} %param.7), kind=kOutput, calls=%fused_computation.84 | convolution fusion | flops 53687091200 | bytes 68157440 | tf_op jit(solution)/shard_map/bsd,bsf->df/dot_general | solution.py:31
  784.7 0.0 reduce-scatter.11.cloned.1.call-start
  784.7 70.8 %fusion.46 = f32[2560,2560]{1,0:T(8,128)} fusion(bf16[1,4096,2560]{2,1,0:T(8,128)(2,1)} %param.9, bf16[2,1,4096,2560]{3,2,1,0:T(8,128)(2,1)} %param.8), kind=kOutput, calls=%fused_computation.63 | convolution fusion | flops 53791948800 | bytes 68157440 | tf_op jit(solution)/shard_map/bsf,bsd->fd/dot_general | solution.py:30
  855.5 0.0 reduce-scatter.9.cloned.1.call-start
  855.6 82.7 %fusion.43 = f32[2560,2560]{1,0:T(8,128)} fusion(bf16[2,1,4096,2560]{3,2,1,0:T(8,128)(2,1)} %param.8, bf16[1,4096,2560]{2,1,0:T(8,128)(2,1)} %all-reduce.3.cloned.1.call-done, bf16[1,4096,2560]{2,1,0:T(8,128)(2,1)} %param.9), kind=kOutput, calls=%fused_computation.61 | convolution fusion | flops 53833891840 | bytes 89128960 | tf_op jit(solution)/shard_map/bsf,bsd->fd/dot_general | solution.py:30
  938.4 63.8 %all-reduce.5.cloned.1.call-done = bf16[1,4096,2560]{2,1,0:T(8,128)(2,1)} async-done(((bf16[1,4096,2560]{2,1,0:T(8,128)(2,1)}), bf16[1,4096,2560]{2,1,0:T(8,128)(2,1)}) %all-reduce.5.cloned.1.call-update) | async-done | bytes 20971536 | tf_op jit(solution)/shard_map/psum | solution.py:28
  1002.1 27.9 %add_convert_fusion = bf16[1,4096,2560]{2,1,0:T(8,128)(2,1)} fusion(bf16[1,4096,2560]{2,1,0:T(8,128)(2,1)} %all-reduce.5.cloned.1.call-done, bf16[1,4096,2560]{2,1,0:T(8,128)(2,1)} %all-reduce.3.cloned.1.call-done, bf16[1,4096,2560]{2,1,0:T(8,128)(2,1)} %param.9), kind=kLoop, calls=%fused_computation.54 | loop fusion | flops 83886080 | bytes 83886080 | tf_op jit(solution)/shard_map/convert_element_type | solution.py:29
  1030.1 266.4 %reduce-scatter.5.cloned.1.call-done = f32[1280,2560]{0,1:T(8,128)} async-done(((f32[2560,2560]{0,1:T(8,128)}), f32[1280,2560]{0,1:T(8,128)}) %reduce-scatter.5.cloned.1.call-update) | async-done | bytes 13107216 | tf_op jit(solution)/shard_map/reduce_scatter | solution.py:33
  1296.5 17.6 pad_maximum_fusion
  1314.1 27.3 %copy.8 = f32[2,1280,2560]{2,1,0:T(8,128)} copy(f32[2,1280,2560]{1,2,0:T(8,128)} %pad_maximum_fusion) | data formatting | bytes 52428800
  1341.4 245.0 %reduce-scatter.11.cloned.1.call-done = f32[2560,1280]{1,0:T(8,128)} async-done(((f32[2560,2560]{1,0:T(8,128)}), f32[2560,1280]{1,0:T(8,128)}) %reduce-scatter.11.cloned.1.call-update) | async-done | bytes 13107216 | tf_op jit(solution)/shard_map/reduce_scatter | solution.py:32
  1586.3 290.0 %reduce-scatter.9.cloned.1.call-done = f32[2560,1280]{1,0:T(8,128)} async-done(((f32[2560,2560]{1,0:T(8,128)}), f32[2560,1280]{1,0:T(8,128)}) %reduce-scatter.9.cloned.1.call-update) | async-done | bytes 13107216 | tf_op jit(solution)/shard_map/reduce_scatter | solution.py:32
  1876.4 17.6 pad_maximum_fusion.1
  (6 shorter events, 0.1 us)
Async XLA Ops:
  8.0 496.9 %all-reduce.3.cloned.1.call-start = ((), (), s32[]{:S(2)}) async-start(), calls=%async_computation.4 | async-start | bytes 41943040 | tf_op jit(solution)/shard_map/psum | solution.py:28
  151.4 850.7 %all-reduce.5.cloned.1.call-start = ((), (), s32[]{:S(2)}) async-start(), calls=%async_computation.5 | async-start | bytes 41943040 | tf_op jit(solution)/shard_map/psum | solution.py:28
  651.4 378.6 %reduce-scatter.7.cloned.1.call-start = ((), (), s32[]{:S(2)}) async-start(), calls=%async_computation.7 | async-start | bytes 39321600 | tf_op jit(solution)/shard_map/reduce_scatter | solution.py:33
  718.2 578.2 %reduce-scatter.5.cloned.1.call-start = ((), (), s32[]{:S(2)}) async-start(), calls=%async_computation.6 | async-start | bytes 39321600 | tf_op jit(solution)/shard_map/reduce_scatter | solution.py:33
  784.7 801.6 %reduce-scatter.11.cloned.1.call-start = ((), (), s32[]{:S(2)}) async-start(), calls=%async_computation.9 | async-start | bytes 39321600 | tf_op jit(solution)/shard_map/reduce_scatter | solution.py:32
  855.5 1020.8 %reduce-scatter.9.cloned.1.call-start = ((), (), s32[]{:S(2)}) async-start(), calls=%async_computation.8 | async-start | bytes 39321600 | tf_op jit(solution)/shard_map/reduce_scatter | solution.py:32
Sparse Core Ops, SparseCore 0:
  151.5 353.3 all-reduce.2
  651.6 350.5 all-reduce.4
Sparse Core Ops, SparseCore 1:
  718.3 287.7 reduce-scatter.6
  1008.8 287.7 reduce-scatter.4
  1298.6 287.7 reduce-scatter.10
  1588.6 287.7 reduce-scatter.8
where the time goes:
time: 1910 us; the launch traced here: 1900 us
  waiting for transfers between devices  1220 us (64%)
  matrix products  576 us (30%)
  other arithmetic  63.1 us (3%)
  local copies, waits for them, and re-layouts  27.3 us (1%)
    reduce_scatter x2, waiting for transfers between devices, local_backward(): lax.psum_scatter(local_down, 'dp', scatter_dimension=1, tiled=True)  535 us
    psum x2, waiting for transfers between devices, local_backward(): full_sum = lax.psum(part_sum, 'tp')  417 us
    reduce_scatter x2, waiting for transfers between devices, local_backward(): lax.psum_scatter(local_up, 'dp', scatter_dimension=0, tiled=True)  266 us
    dot_general x2, matrix products, local_backward(): jnp.einsum('bsd,fd->bsf', grad_cur, w_down[layer_idx], preferred_element_...  164 us
    dot_general x2, matrix products, local_backward(): jnp.einsum('bsf,bsd->fd', act_val.astype(jnp.bfloat16), grad_cur, preferr...  154 us
    dot_general x2, matrix products, local_backward(): jnp.einsum('bsd,bsf->df', saved_x[layer_idx], d_pre, preferred_element_ty...  133 us
    dot_general x2, matrix products, local_backward(): jnp.einsum('bsf,df->bsd', d_pre, w_up[layer_idx], preferred_element_type=...  126 us
  transfers between devices with their start and end apart: 6, of which 5 were waited for; matrix products, arithmetic and copies ran while one was open for 19% of the time, Pallas kernels for 0%

commit v1 on v0

v1 whole, which is shorter than its diff:
```python
import math

import jax
import jax.numpy as jnp
from jax import lax
from jax.experimental import pallas as pl
from jax.experimental.pallas import tpu as pltpu
from jax.sharding import PartitionSpec as P

C0 = math.sqrt(2.0 / math.pi)
C1 = 0.044715
F32, BF16 = jnp.float32, jnp.bfloat16
ANY = pl.BlockSpec(memory_space=pl.ANY)
VMEM_LIMIT = 67043328
BM = 512


def gelu_and_slope(h):
    sq = h * h
    q = 0.5 + 0.5 * jnp.tanh(h * (C0 + (C0 * C1) * sq))
    act = h * q
    return act, q + act * (1.0 - q) * (2.0 * C0 + (6.0 * C0 * C1) * sq)


def dot(a, b, ca, cb):
    return lax.dot_general(a, b, (((ca,), (cb,)), ((), ())), preferred_element_type=F32)


def dw_step(kind, acc, lr, rr):
    n = acc.shape[1]
    for i in range(2):
        at = slice(i * n, i * n + n)
        if kind == "up":
            acc[i] += dot(lr[...], rr[:, at], 0, 0)
        else:
            acc[i] += dot(lr[:, at], rr[...], 0, 0)


def halves(kind, ref, i, n):
    at = pl.ds(i * n, n)
    return ref.at[:, at] if kind == "up" else ref.at[at]


def main_kernel(
    w_up, w_down, xs, hs, g2,
    g0, g1, dh, aa, ps, r1, r2, xp1, gp2, xp0, gp1, dhp, ap, down1, up1, down0, up0,
    wu, wd, acc, wsem, asem, send, recv,
):
    tokens, width = g2.shape[1:]
    dp, tp = lax.axis_index("dp"), lax.axis_index("tp")
    c, x = lax.rem(tp, 2), lax.div(tp, 2)
    Y, X, C = (1 - dp, tp), (dp, (1 - x) * 2 + c), (dp, x * 2 + (1 - c))
    half = tokens // 2
    quarter = tokens // 4
    sub = quarter // 2
    NB = width // 2

    barrier = pltpu.get_barrier_semaphore()
    for peer in (Y, X, C):
        pl.semaphore_signal(barrier, inc=1, device_id=peer, device_id_type=pl.DeviceIdType.MESH)
    pl.semaphore_wait(barrier, 3)

    slot = {}

    def rc(name, src, dst, to, s=0, n=1):
        if name not in slot:
            slot[name] = sum(v[1] for v in slot.values()), n
        i = slot[name][0] + s
        return pltpu.make_async_remote_copy(
            src_ref=src, dst_ref=dst, send_sem=send.at[i], recv_sem=recv.at[i],
            device_id=to, device_id_type=pl.DeviceIdType.MESH)

    def at_rows(ref, start, size):
        return ref.at[pl.ds(pl.multiple_of(start, sub), size)]

    def qrow(cc, xx, s):
        return cc * half + xx * quarter + s * sub

    def same(name, src, dst, row, to, s=0, n=1):
        return rc(name, at_rows(src, row, sub), at_rows(dst, row, sub), to, s, n)

    def k_row(k):
        return c * half + k * sub

    x1, x0, gtop = xs.at[1, 0], xs.at[0, 0], g2.at[0]

    def kx(k):
        return same(f"kx{k}", x1, xp1, k_row(k), Y)

    def kg(k):
        return same(f"kg{k}", gtop, gp2, k_row(k), Y)

    def fkx(k):
        return same(f"fkx{k}", xp1, xp1, k_row(k), C)

    def fkg(k):
        return same(f"fkg{k}", gp2, gp2, k_row(k), C)

    def share(tag, src, dst):
        return {
            "y": lambda s: same(f"{tag}y{s}", src, dst, qrow(c, x, s), Y),
            "x": lambda s: same(f"{tag}x{s}", dst, dst, qrow(c, x, s), X),
            "c": lambda s: same(f"{tag}c{s}", dst, dst, qrow(c, x, s), C),
            "f": lambda s: same(f"{tag}f{s}", dst, dst, qrow(c, 1 - x, s), C),
        }

    sx0 = share("sx0", x0, xp0)
    sg1 = share("sg1", g1, gp1)

    def gather(tag, g):
        return {
            "x": lambda s: same(f"{tag}x{s}", g, g, qrow(c, x, s), X),
            "c": lambda s: same(f"{tag}c{s}", g, g, qrow(c, x, s), C),
            "f": lambda s: same(f"{tag}f{s}", g, g, qrow(c, 1 - x, s), C),
        }

    ag = {1: gather("ag1", g1), 0: gather("ag0", g0)}

    def r1_copy(l, pair):
        xx = jnp.where(pair < 2, 1 - x, x)
        s = lax.rem(pair, 2)
        return rc(f"r1_{l}", at_rows(ps.at[l], qrow(1 - c, xx, s), sub),
                  at_rows(r1.at[l], xx * quarter + s * sub, sub), C, pair, 4)

    def r2_copy(l, s):
        return rc(f"r2_{l}", at_rows(ps.at[l], qrow(c, 1 - x, s), sub),
                  at_rows(r2.at[l], s * sub, sub), X, s, 2)

    def load(l, which):
        src, dst, i = (w_up, wu, 0) if which == "up" else (w_down, wd, 1)
        return pltpu.make_async_copy(src.at[l], dst, wsem.at[i])

    def d_act(l, g, blk):
        def body(gr, hr, dr, ar):
            n = pl.program_id(1)
            d = dot(gr[...], wd[pl.ds(pl.multiple_of(n * NB, NB), NB), :], 1, 1)
            act, slope = gelu_and_slope(hr[...].astype(F32))
            dr[...] = (d * slope).astype(BF16)
            ar[...] = act.astype(BF16)

        tile = pl.BlockSpec((BM, NB), lambda i, n: (blk + i, n))
        pltpu.emit_pipeline(
            body, grid=(1, 2),
            in_specs=[pl.BlockSpec((BM, width), lambda i, n: (blk + i, 0)), tile],
            out_specs=[tile, tile],
        )(g, hs.at[l, 0], dh.at[l], aa.at[l])

    def d_x(l, blk, add_blk=None):
        def body(dr, *rest):
            n = pl.program_id(1)
            out = dot(dr[...], wu[pl.ds(pl.multiple_of(n * NB, NB), NB), :], 1, 1)
            if len(rest) == 2:
                out = out + rest[0][...].astype(F32)
            rest[-1][...] = out.astype(BF16)

        tile = pl.BlockSpec((BM, NB), lambda i, n: (blk + i, n))
        ins = [pl.BlockSpec((BM, width), lambda i, n: (blk + i, 0))]
        refs = [dh.at[l]]
        if add_blk is not None:
            ins.append(pl.BlockSpec((BM, NB), lambda i, n: (add_blk + i, n)))
            refs.append(r1.at[l])
        pltpu.emit_pipeline(body, grid=(1, 2), in_specs=ins, out_specs=[tile])(*refs, ps.at[l])

    def own(l, g, hook):
        def pair_step(pair, _):
            xx = jnp.where(pair < 2, 1 - x, x)
            s = lax.rem(pair, 2)
            other = (1 - c) * 4 + xx * 2 + s
            mine = c * 4 + xx * 2 + s

            def step(j, _):
                blk = jnp.where(j == 0, other, mine)
                if l == 0:
                    @pl.when(jnp.logical_and(pair < 2, j == 0))
                    def _():
                        @pl.when(s == 0)
                        def _():
                            ag[1]["f"](0).wait_recv()

                        @pl.when(s == 1)
                        def _():
                            ag[1]["f"](1).wait_recv()
                d_act(l, g, blk)

                @pl.when(j == 0)
                def _():
                    d_x(l, blk)
                    r1_copy(l, pair).start()

                @pl.when(j == 1)
                def _():
                    r1_copy(l, pair).wait_recv()
                    d_x(l, blk, xx * 2 + s)

                    @pl.when(pair < (2 if l == 1 else 1))
                    def _():
                        r2_copy(l, s).start()
                return 0

            lax.fori_loop(0, 2, step, 0)
            for p in range(4):
                @pl.when(pair == p)
                def _():
                    hook(p)
            return 0

        lax.fori_loop(0, 4, pair_step, 0)

    QB = 128

    def add_quarter(l, g, out, s):
        r2_copy(l, s).wait_recv()
        base = lax.div(qrow(c, x, s), QB)

        def body(gr, pr, rr, orf):
            orf[...] = (gr[...].astype(F32) + (pr[...].astype(F32) + rr[...].astype(F32))).astype(BF16)

        at = pl.BlockSpec((QB, width), lambda i: (base + i, 0))
        pltpu.emit_pipeline(
            body, grid=(sub // QB,),
            in_specs=[at, at, pl.BlockSpec((QB, width), lambda i: (s * (sub // QB) + i, 0))],
            out_specs=[at],
        )(g, ps.at[l], r2.at[l], out)
        ag[l]["c"](s).start()

    def peer(l, px, pg, blocks, row_block):
        def body(xr, gr, dr, ar):
            n = pl.program_id(1)
            t = pl.ds(pl.multiple_of(n * NB, NB), NB)
            pre = dot(xr[...], wu[:, t], 1, 0).astype(BF16)
            act, slope = gelu_and_slope(pre.astype(F32))
            ar[...] = act.astype(BF16)
            dr[...] = (dot(gr[...], wd[t, :], 1, 1) * slope).astype(BF16)

        full = pl.BlockSpec((BM, width), lambda i, n: (row_block(i), 0))
        tile = pl.BlockSpec((BM, NB), lambda i, n: (row_block(i), n))
        pltpu.emit_pipeline(body, grid=(blocks, 2), in_specs=[full, full], out_specs=[tile, tile])(
            px, pg, dhp.at[l], ap.at[l])

    def acc_copies(kind, ref, out):
        res = []
        for i in range(2):
            far = halves(kind, ref, i, NB) if kind else ref.at[i]
            pair = (acc.at[i], far) if out else (far, acc.at[i])
            res.append(pltpu.make_async_copy(*pair, asem.at[i]))
        return res

    def weights(kind, dst, init, lhs, rhs, blocks, row_block, final=True):
        lay = kind if final else None
        if init:
            for cp in acc_copies(lay, dst, False):
                cp.start()
            for cp in acc_copies(lay, dst, False):
                cp.wait()
        else:
            acc[...] = jnp.zeros_like(acc)
        lw, rw = (NB, width) if kind == "up" else (width, NB)
        lcol, rcol = (dp, 0) if kind == "up" else (0, dp)
        pltpu.emit_pipeline(
            lambda lr, rr: dw_step(kind, acc, lr, rr),
            grid=(blocks,),
            in_specs=[
                pl.BlockSpec((BM, lw), lambda i: (row_block(i), lcol)),
                pl.BlockSpec((BM, rw), lambda i: (row_block(i), rcol)),
            ],
        )(lhs, rhs)
        for cp in acc_copies(lay, dst, True):
            cp.start()
        for cp in acc_copies(lay, dst, True):
            cp.wait()

    def all_rows(i):
        return i

    def k_blocks(k):
        return lambda i: i * 4 + k

    kx(0).start()
    kg(0).start()
    load(1, "down").start()
    load(1, "up").start()
    load(1, "down").wait()
    load(1, "up").wait()

    def hook1(p):
        if p == 2:
            kx(1).start()
            kg(1).start()

    own(1, gtop, hook1)
    kx(0).wait_recv()
    kg(0).wait_recv()
    fkx(0).start()
    fkg(0).start()
    add_quarter(1, gtop, g1, 0)
    ag[1]["x"](0).start()
    weights("down", down1, False, aa.at[1], gtop, 8, all_rows, False)
    add_quarter(1, gtop, g1, 1)
    ag[1]["x"](1).start()
    weights("up", up1, False, x1, dh.at[1], 8, all_rows, False)
    for s in range(2):
        sx0["y"](s).start()
    fkx(0).wait_recv()
    fkg(0).wait_recv()
    ag[1]["x"](0).wait_recv()
    ag[1]["f"](0).start()
    peer(1, xp1, gp2, 2, k_blocks(0))
    kx(1).wait_recv()
    kg(1).wait_recv()
    fkx(1).start()
    fkg(1).start()
    fkx(1).wait_recv()
    fkg(1).wait_recv()
    peer(1, xp1, gp2, 2, k_blocks(1))
    load(0, "down").start()
    load(0, "up").start()
    ag[1]["x"](1).wait_recv()
    ag[1]["f"](1).start()
    for s in range(2):
        ag[1]["c"](s).wait_recv()
    def pass_on(sh, s):
        sh["y"](s).wait_recv()
        sh["x"](s).start()
        sh["c"](s).start()

    def pass_core(sh, s):
        sh["x"](s).wait_recv()
        sh["f"](s).start()

    def have(s):
        for sh in (sx0, sg1):
            for kind in "cf":
                sh[kind](s).wait_recv()

    def hook0(p):
        if p == 1:
            pass_on(sx0, 1)
        if p == 2:
            pass_core(sx0, 0)

    pass_on(sx0, 0)
    for s in range(2):
        sg1["y"](s).start()
    load(0, "down").wait()
    load(0, "up").wait()
    own(0, g1, hook0)
    pass_on(sg1, 0)
    kx(2).start()
    kg(2).start()
    weights("down", down0, False, aa.at[0], g1, 8, all_rows, False)
    add_quarter(0, g1, g0, 0)
    weights("up", up0, False, x0, dh.at[0], 8, all_rows, False)
    pass_on(sg1, 1)
    r2_copy(0, 1).start()
    ag[0]["x"](0).start()
    pass_core(sx0, 1)
    early = lambda i: lax.div(i, 2) * 4 + lax.rem(i, 2)
    late = lambda i: lax.div(i, 2) * 4 + 2 + lax.rem(i, 2)
    weights("down", down1, True, ap.at[1], gp2, 4, early, False)
    pass_core(sg1, 0)
    kx(3).start()
    kg(3).start()
    have(0)
    peer(0, xp0, gp1, 4, lambda i: i * 2)
    pass_core(sg1, 1)
    kx(2).wait_recv()
    kg(2).wait_recv()
    fkx(2).start()
    fkg(2).start()
    have(1)
    peer(0, xp0, gp1, 4, lambda i: i * 2 + 1)
    load(1, "down").start()
    load(1, "up").start()
    add_quarter(0, g1, g0, 1)
    ag[0]["x"](1).start()
    fkx(2).wait_recv()
    fkg(2).wait_recv()
    load(1, "down").wait()
    load(1, "up").wait()
    peer(1, xp1, gp2, 2, k_blocks(2))
    weights("up", up1, True, xp1, dhp.at[1], 4, early, False)
    kx(3).wait_recv()
    kg(3).wait_recv()
    fkx(3).start()
    fkg(3).start()
    ag[0]["x"](0).wait_recv()
    ag[0]["f"](0).start()
    fkx(3).wait_recv()
    fkg(3).wait_recv()
    peer(1, xp1, gp2, 2, k_blocks(3))
    weights("down", down1, True, ap.at[1], gp2, 4, late, False)
    weights("up", up1, True, xp1, dhp.at[1], 4, late, False)
    ag[0]["x"](1).wait_recv()
    ag[0]["f"](1).start()
    for s in range(2):
        ag[0]["c"](s).wait_recv()
        ag[0]["f"](s).wait_recv()

    for k in range(4):
        for d in (kx, kg, fkx, fkg):
            d(k).wait_send()
    for l in range(2):
        for pair in range(4):
            r1_copy(l, pair).wait_send()
        for s in range(2):
            r2_copy(l, s).wait_send()
            for kind in "xcf":
                ag[l][kind](s).wait_send()
    for sh in (sx0, sg1):
        for kind in "yxcf":
            for s in range(2):
                sh[kind](s).wait_send()


N_COPIES = 64


def finish_kernel(xp0, gp1, dhp, ap, down0, up0, down1, up1, g0_in, g0, dw_up, dw_down, acc_d, acc_u, sem):
    dp = lax.axis_index("dp")
    tokens, width = g0_in.shape
    NB = width // 2
    blocks = tokens // BM
    ins = [pltpu.make_async_copy(src, dst, sem.at[i]) for i, (src, dst) in enumerate(((down0, acc_d), (up0, acc_u)))]
    for cp in ins:
        cp.start()

    def phase(kind, acc, lhs, rhs, moved, out, g_at):
        lw, rw = (NB, width) if kind == "up" else (width, NB)
        lcol, rcol = (dp, 0) if kind == "up" else (0, dp)
        rows = 2 * NB // blocks
        gb = tokens // (2 * blocks)

        def body(lr, rr, mr, gr, mo, go):
            dw_step(kind, acc, lr, rr)
            mo[...] = mr[0] if len(mr.shape) == 3 else mr[...]
            go[...] = gr[...]

        half = blocks // 2
        if kind == "up":
            out_spec = pl.BlockSpec((rows, NB), lambda i: (lax.rem(i, half), lax.div(i, half)))
        else:
            out_spec = pl.BlockSpec((rows, NB), lambda i: (i, 0))
        g_spec = pl.BlockSpec((gb, width), lambda i: (g_at * blocks + i, 0))
        pltpu.emit_pipeline(
            body, grid=(blocks,),
            in_specs=[
                pl.BlockSpec((BM, lw), lambda i: (i, lcol)),
                pl.BlockSpec((BM, rw), lambda i: (i, rcol)),
                pl.BlockSpec((1, rows, NB), lambda i: (lax.div(i, half), lax.rem(i, half), 0)),
                g_spec,
            ],
            out_specs=[out_spec, g_spec],
        )(lhs, rhs, moved, g0_in, out, g0.at[0])

    def put(kind, acc, dst):
        return [pltpu.make_async_copy(acc.at[i], halves(kind, dst, i, NB), sem.at[2 * (kind == "up") + i]) for i in range(2)]

    ins[0].wait()
    phase("down", acc_d, ap.at[0], gp1, down1, dw_down.at[1], 0)
    ins[1].wait()
    outs = put("down", acc_d, dw_down.at[0])
    for cp in outs:
        cp.start()
    phase("up", acc_u, xp0, dhp.at[0], up1, dw_up.at[1], 1)
    outs += put("up", acc_u, dw_up.at[0])
    for cp in outs[2:]:
        cp.start()
    for cp in outs:
        cp.wait()


def solution(mesh):
    def local_backward(w_up, w_down, saved_x, saved_h, grad_out):
        tokens, width = grad_out.shape[1:]
        row = jax.ShapeDtypeStruct((tokens, width), BF16)
        two = jax.ShapeDtypeStruct((2, tokens, width), BF16)
        half = jax.ShapeDtypeStruct((2, tokens // 2, width), BF16)
        quarter = jax.ShapeDtypeStruct((2, tokens // 4, width), BF16)
        sums = jax.ShapeDtypeStruct((2, width // 2, width // 2), F32)
        outs = [row, row, two, two, two, half, quarter, row, row, row, row, two, two, sums, sums, sums, sums]
        flops = 2 * tokens * width * width
        g0, g1, dh, aa, ps, r1, r2, xp1, gp2, xp0, gp1, dhp, ap, down1, up1, down0, up0 = pl.pallas_call(
            main_kernel,
            out_shape=outs,
            in_specs=[ANY] * 5,
            out_specs=[ANY] * len(outs),
            scratch_shapes=[
                pltpu.VMEM((width, width), BF16),
                pltpu.VMEM((width, width), BF16),
                pltpu.VMEM(sums.shape, F32),
                pltpu.SemaphoreType.DMA((2,)),
                pltpu.SemaphoreType.DMA((2,)),
                pltpu.SemaphoreType.DMA((N_COPIES,)),
                pltpu.SemaphoreType.DMA((N_COPIES,)),
            ],
            compiler_params=pltpu.CompilerParams(
                collective_id=0, has_side_effects=True, vmem_limit_bytes=VMEM_LIMIT),
            cost_estimate=pl.CostEstimate(flops=11 * flops, bytes_accessed=10**9, transcendentals=0),
            name="backward_main",
        )(w_up, w_down, saved_x, saved_h, grad_out)
        return tuple(pl.pallas_call(
            finish_kernel,
            out_shape=[
                jax.ShapeDtypeStruct((1, tokens, width), BF16),
                jax.ShapeDtypeStruct((2, width // 2, width), F32),
                jax.ShapeDtypeStruct((2, width, width // 2), F32),
            ],
            in_specs=[ANY] * 9,
            out_specs=[ANY] * 3,
            scratch_shapes=[
                pltpu.VMEM(sums.shape, F32),
                pltpu.VMEM(sums.shape, F32),
                pltpu.SemaphoreType.DMA((4,)),
            ],
            compiler_params=pltpu.CompilerParams(vmem_limit_bytes=VMEM_LIMIT),
            cost_estimate=pl.CostEstimate(flops=flops, bytes_accessed=3 * 10**8, transcendentals=0),
            name="backward_finish",
        )(xp0, gp1, dhp, ap, down0, up0, down1, up1, g0))

    return jax.shard_map(
        local_backward,
        mesh=mesh,
        in_specs=(P(None, None, "tp"), P(None, "tp", None), P(None, "dp", None, None), P(None, "dp", None, "tp"), P("dp", None, None)),
        out_specs=(P("dp", None, None), P(None, "dp", "tp"), P(None, "tp", "dp")),
        check_vma=False,
    )
```

time: 1910 us -> 1040 us (0.54)
  waiting for transfers between devices: 1220 us -> 0 us
  Pallas kernels: 0 us -> 1030 us
  matrix products: 576 us -> 0 us
  other arithmetic: 63.1 us -> 0 us
  local copies, waits for them, and re-layouts: 27.3 us -> 0 us
    pallas_call x0 -> x2, Pallas kernels: none -> 1030 us  [the longest x1 944 us: local_backward(): pl.pallas_call(main_kernel, out_shape=outs, in_specs=[ANY] * 5, out_specs...]
    reduce_scatter x4 -> x0, waiting for transfers between devices: 801 us -> none  [the longest x2 535 us: local_backward(): lax.psum_scatter(local_down, 'dp', scatter_dimension=1, tiled=True)]
    dot_general x8 -> x0, matrix products: 576 us -> none  [the longest x2 164 us: local_backward(): jnp.einsum('bsd,fd->bsf', grad_cur, w_down[layer_idx], preferred_element_...]
    psum x2 -> x0, waiting for transfers between devices: 417 us -> none  [local_backward(): full_sum = lax.psum(part_sum, 'tp')]
    another operation x2 -> x0, other arithmetic: 35.2 us -> none  [local_backward(): return (grad_cur, jnp.stack(up_list[::-1]), jnp.stack(down_list[::-1]))]
    convert_element_type x1 -> x0, other arithmetic: 27.9 us -> none  [local_backward(): (grad_cur.astype(jnp.float32) + full_sum.astype(jnp.float32)).astype(jnp....]
    unnamed x1 -> x0, local copies, waits for them, and re-layouts: 27.3 us -> none
  transfers between devices with their start and end apart: 6 -> 0, of which waited for: 5 -> 0; matrix products, arithmetic and copies ran while one was open for 19% -> 0% of each run, Pallas kernels for 0% -> 0%
where the time goes in v1:
time: 1040 us; the launch traced here: 1030 us
  Pallas kernels  1030 us (99%)
    pallas_call x1, Pallas kernels, local_backward(): pl.pallas_call(main_kernel, out_shape=outs, in_specs=[ANY] * 5, out_specs...  944 us
    pallas_call x1, Pallas kernels, local_backward(): pl.pallas_call(finish_kernel, out_shape=[jax.ShapeDtypeStruct((1, tokens,...  88.5 us

profile of v1, /device:TPU:0, one launch (start us, length us, event | category | flops | bytes accessed | tf_op | source)
XLA Modules:
  0.0 1034.1 jit_solution(16357960389022093798)
XLA Ops:
  0.6 944.4 %backward_main.1 = (bf16[4096,2560]{1,0:T(8,128)(2,1)}, bf16[4096,2560]{1,0:T(8,128)(2,1)}, bf16[2,4096,2560]{2,1,0:T(8,128)(2,1)}, bf16[2,4096,2560]{2,1,0:T(8,...) custom-call(bf16[2,2560,2560]{2,1,0:T(8,128)(2,1)} %w_up.1, ...), custom_call_target="tpu_custom_call" | custom-call | flops 590558003200 | bytes 1000000000 | tf_op jit(solution)/shard_map/backward_main/pallas_call | solution.py:482
  945.0 88.5 %backward_finish.1 = (bf16[1,4096,2560]{2,1,0:T(8,128)(2,1)}, f32[2,1280,2560]{2,1,0:T(8,128)}, f32[2,2560,1280]{2,1,0:T(8,128)}) custom-call(bf16[4096,2560]{1,0:T(8,128)(2,1)} %get-tuple-element.12.xp0, bf16[4096,2560]{1,0:T(8,128)(2,1)} %get-tuple-element.13.gp1, bf16[2,4096,2560]{2,1,0:T(8,128)(2,1)} %get-tuple-element.14.dhp, ...), custom_call_target="tpu_custom_call" | custom-call | flops 53687091200 | bytes 300000000 | tf_op jit(solution)/shard_map/backward_finish/pallas_call | solution.py:501

commit v2 on v1

v2 whole, which is shorter than its diff:
```python
import math

import jax
import jax.numpy as jnp
from jax import lax
from jax.experimental import pallas as pl
from jax.experimental.pallas import tpu as pltpu
from jax.sharding import PartitionSpec as P

C0 = math.sqrt(2.0 / math.pi)
C1 = 0.044715
F32, BF16 = jnp.float32, jnp.bfloat16
ANY = pl.BlockSpec(memory_space=pl.ANY)
VMEM_LIMIT = 67043328
BM = 512


def gelu_and_slope(h):
    sq = h * h
    q = 0.5 + 0.5 * jnp.tanh(h * (C0 + (C0 * C1) * sq))
    act = h * q
    return act, q + act * (1.0 - q) * (2.0 * C0 + (6.0 * C0 * C1) * sq)


def dot(a, b, ca, cb):
    return lax.dot_general(a, b, (((ca,), (cb,)), ((), ())), preferred_element_type=F32)


def dw_step(kind, acc, lr, rr):
    n = acc.shape[1]
    for i in range(2):
        at = slice(i * n, i * n + n)
        if kind == "up":
            acc[i] += dot(lr[...], rr[:, at], 0, 0)
        else:
            acc[i] += dot(lr[:, at], rr[...], 0, 0)


def halves(kind, ref, i, n):
    at = pl.ds(i * n, n)
    return ref.at[:, at] if kind == "up" else ref.at[at]


def main_kernel(
    w_up, w_down, xs, hs, g2,
    g0, g1, dh, aa, ps, r2, xp1, gp2, xp0, gp1, dhp, ap, down1, up1, down0, up0,
    wu, wd, add_buf, wsem, asem, psem, send, recv,
):
    tokens, width = g2.shape[1:]
    dp, tp = lax.axis_index("dp"), lax.axis_index("tp")
    c, x = lax.rem(tp, 2), lax.div(tp, 2)
    Y, X, C = (1 - dp, tp), (dp, (1 - x) * 2 + c), (dp, x * 2 + (1 - c))
    half = tokens // 2
    quarter = tokens // 4
    sub = quarter // 2
    NB = width // 2

    def load(l, which):
        src, dst, i = (w_up, wu, 0) if which == "up" else (w_down, wd, 1)
        return pltpu.make_async_copy(src.at[l], dst, wsem.at[i])

    load(1, "down").start()
    load(1, "up").start()
    add_buf[1] = jnp.zeros(add_buf.shape[1:], BF16)
    barrier = pltpu.get_barrier_semaphore()
    for peer in (Y, X, C):
        pl.semaphore_signal(barrier, inc=1, device_id=peer, device_id_type=pl.DeviceIdType.MESH)
    pl.semaphore_wait(barrier, 3)

    slot = {}

    def rc(name, src, dst, to, s=0, n=1):
        if name not in slot:
            slot[name] = sum(v[1] for v in slot.values()), n
        i = slot[name][0] + s
        return pltpu.make_async_remote_copy(
            src_ref=src, dst_ref=dst, send_sem=send.at[i], recv_sem=recv.at[i],
            device_id=to, device_id_type=pl.DeviceIdType.MESH)

    def at_rows(ref, start, size):
        return ref.at[pl.ds(pl.multiple_of(start, sub), size)]

    def qrow(cc, xx, s):
        return cc * half + xx * quarter + s * sub

    def same(name, src, dst, row, to, s=0, n=1):
        return rc(name, at_rows(src, row, sub), at_rows(dst, row, sub), to, s, n)

    def k_row(k):
        return c * half + k * sub

    x1, x0, gtop = xs.at[1, 0], xs.at[0, 0], g2.at[0]

    def kx(k):
        return same(f"kx{k}", x1, xp1, k_row(k), Y)

    def kg(k):
        return same(f"kg{k}", gtop, gp2, k_row(k), Y)

    def fkx(k):
        return same(f"fkx{k}", xp1, xp1, k_row(k), C)

    def fkg(k):
        return same(f"fkg{k}", gp2, gp2, k_row(k), C)

    def share(tag, src, dst):
        return {
            "y": lambda s: same(f"{tag}y{s}", src, dst, qrow(c, x, s), Y),
            "x": lambda s: same(f"{tag}x{s}", dst, dst, qrow(c, x, s), X),
            "c": lambda s: same(f"{tag}c{s}", dst, dst, qrow(c, x, s), C),
            "f": lambda s: same(f"{tag}f{s}", dst, dst, qrow(c, 1 - x, s), C),
        }

    sx0 = share("sx0", x0, xp0)
    sg1 = share("sg1", g1, gp1)

    def gather(tag, g):
        return {
            "x": lambda s: same(f"{tag}x{s}", g, g, qrow(c, x, s), X),
            "c": lambda s: same(f"{tag}c{s}", g, g, qrow(c, x, s), C),
            "f": lambda s: same(f"{tag}f{s}", g, g, qrow(c, 1 - x, s), C),
        }

    ag = {1: gather("ag1", g1), 0: gather("ag0", g0)}

    def half_cols(m):
        return pl.ds(m * NB, NB)

    def r1_copy(l, pair, m, share_buf):
        return rc(f"r1_{l}", share_buf.at[m], add_buf.at[lax.rem(pair, 2), m], C, pair * 2 + m, 8)

    def r2_copy(l, s):
        return rc(f"r2_{l}", at_rows(ps.at[l], qrow(c, 1 - x, s), sub),
                  at_rows(r2.at[l], s * sub, sub), X, s, 2)

    def at_step(cond, hook):
        @pl.when(cond)
        def _():
            hook()

    def own(l, g, hooks, dh_even, dh_odd, share_buf):
        def place(i):
            pair, j = lax.div(i, 2), lax.rem(i, 2)
            xx = jnp.where(pair < 2, 1 - x, x)
            return pair, j, jnp.where(j == 0, 1 - c, c) * 4 + xx * 2 + lax.rem(pair, 2)

        def kept(blk, m):
            rows = pl.ds(pl.multiple_of(blk * BM, BM), BM)
            return pltpu.make_async_copy(share_buf.at[m], ps.at[l, rows, half_cols(m)], psem.at[m])

        def act_part(n, keep, gr, hr, dr, ar):
            at = pl.ds(pl.multiple_of(n * NB, NB), NB)
            d = dot(gr[...], wd[at, :], 1, 1)
            act, slope = gelu_and_slope(hr[...].astype(F32))
            d = (d * slope).astype(BF16)
            keep[:, at] = d
            dr[...] = d
            ar[...] = act.astype(BF16)

        def x_part(b, n, kept_dh):
            pair, j, _ = place(b)
            at = pl.ds(pl.multiple_of(n * NB, NB), NB)
            out = dot(kept_dh[...], wu[at, :], 1, 1)
            got = add_buf[jnp.where(j == 1, lax.rem(pair, 2), 1 - lax.rem(pair, 2)), n].astype(F32)
            share_buf[n] = (out + jnp.where(j == 1, got, 0.0)).astype(BF16)

        def body(gr, hr, dr, ar):
            i, n = pl.program_id(0), pl.program_id(1)
            b = i - 1
            pair, j, blk = place(b)

            @pl.when(jnp.logical_and(i > 0, j == 1))
            def _():
                r1_copy(l, pair, n, share_buf).wait_recv()
                r1_copy(l, pair, n, share_buf).wait_send()

            @pl.when(jnp.logical_and(j == 0, i > 1))
            def _():
                kept(place(b - 1)[2], n).wait()

                if l == 1:
                    @pl.when(jnp.logical_and(n == 1, pair - 1 < 2))
                    def _():
                        r2_copy(l, lax.rem(pair - 1, 2)).start()

            if l == 0:
                @pl.when(jnp.logical_and(i == 1, n == 0))
                def _():
                    ag[1]["f"](1).wait_recv()

            @pl.when(jnp.logical_and(i == 1, n == 0))
            def _():
                load(l, "up").wait()

            @pl.when(i == 0)
            def _():
                act_part(n, dh_even, gr, hr, dr, ar)

            for odd, (new, old) in enumerate(((dh_even, dh_odd), (dh_odd, dh_even))):
                @pl.when(jnp.logical_and(lax.rem(i, 2) == odd, jnp.logical_and(i > 0, i < 8)))
                def _():
                    act_part(n, new, gr, hr, dr, ar)
                    x_part(b, n, old)

            @pl.when(i == 8)
            def _():
                x_part(b, n, dh_odd)

            @pl.when(jnp.logical_and(i > 0, j == 0))
            def _():
                r1_copy(l, pair, n, share_buf).start()

            @pl.when(jnp.logical_and(i > 0, j == 1))
            def _():
                kept(blk, n).start()

            for at_i, hook in hooks.items():
                at_step(jnp.logical_and(i == at_i, n == 1), hook)

        def act_block(i):
            return place(jnp.minimum(i, 7))[2]

        tile = pl.BlockSpec((BM, NB), lambda i, n: (act_block(i), jnp.where(i == 8, 1, n)))
        pltpu.emit_pipeline(
            body, grid=(9, 2),
            in_specs=[pl.BlockSpec((BM, width), lambda i, n: (act_block(i), 0)), tile],
            out_specs=[tile, tile],
        )(g, hs.at[l, 0], dh.at[l], aa.at[l])
        for m in range(2):
            kept(place(7)[2], m).wait()

    def run_own(l, g, hooks):
        pl.run_scoped(
            lambda *bufs: own(l, g, hooks, *bufs),
            pltpu.VMEM((BM, width), BF16), pltpu.VMEM((BM, width), BF16), pltpu.VMEM((2, BM, NB), BF16))

    QB = 128

    def add_quarter(l, g, out, s):
        r2_copy(l, s).wait_recv()
        base = lax.div(qrow(c, x, s), QB)

        def body(gr, pr, rr, orf):
            orf[...] = (gr[...].astype(F32) + (pr[...].astype(F32) + rr[...].astype(F32))).astype(BF16)

        at = pl.BlockSpec((QB, width), lambda i: (base + i, 0))
        pltpu.emit_pipeline(
            body, grid=(sub // QB,),
            in_specs=[at, at, pl.BlockSpec((QB, width), lambda i: (s * (sub // QB) + i, 0))],
            out_specs=[at],
        )(g, ps.at[l], r2.at[l], out)
        ag[l]["c"](s).start()

    def peer(l, px, pg, blocks, row_block, hooks={}):
        def body(xr, gr, dr, ar):
            i, n = pl.program_id(0), pl.program_id(1)
            for at_i, hook in hooks.items():
                at_step(jnp.logical_and(i == at_i, n == 0), hook)
            t = pl.ds(pl.multiple_of(n * NB, NB), NB)
            pre = dot(xr[...], wu[:, t], 1, 0).astype(BF16)
            act, slope = gelu_and_slope(pre.astype(F32))
            ar[...] = act.astype(BF16)
            dr[...] = (dot(gr[...], wd[t, :], 1, 1) * slope).astype(BF16)

        full = pl.BlockSpec((BM, width), lambda i, n: (row_block(i), 0))
        tile = pl.BlockSpec((BM, NB), lambda i, n: (row_block(i), n))
        pltpu.emit_pipeline(body, grid=(blocks, 2), in_specs=[full, full], out_specs=[tile, tile])(
            px, pg, dhp.at[l], ap.at[l])

    pending = {0: [], 1: []}

    def acc_copies(acc, which, ref, out):
        pairs = [(acc.at[i], ref.at[i]) if out else (ref.at[i], acc.at[i]) for i in range(2)]
        return [pltpu.make_async_copy(*pair, asem.at[which * 2 + i]) for i, pair in enumerate(pairs)]

    def settle(which):
        for args in pending[which]:
            for cp in acc_copies(*args):
                cp.wait()
        pending[which] = []

    def move(acc, which, ref, out):
        settle(which)
        pending[which] = [(acc, which, ref, out)]
        for cp in acc_copies(acc, which, ref, out):
            cp.start()

    def weights(kind, acc, which, lhs, rhs, blocks, row_block, zero=False, hooks={}, split=False):
        settle(which)
        if zero:
            acc[...] = jnp.zeros_like(acc)
        up = kind == "up"
        if split:
            def body(lr, rr):
                i, n = pl.program_id(0), pl.program_id(1)
                for at_i, hook in hooks.items():
                    at_step(jnp.logical_and(i == at_i, n == 0), hook)
                acc[n] += dot(lr[...], rr[...], 0, 0)

            pltpu.emit_pipeline(
                body,
                grid=(blocks, 2),
                in_specs=[
                    pl.BlockSpec((BM, NB), lambda i, n: (row_block(i), dp if up else n)),
                    pl.BlockSpec((BM, NB), lambda i, n: (row_block(i), n if up else dp)),
                ],
            )(lhs, rhs)
            return
        lw, rw = (NB, width) if up else (width, NB)
        lcol, rcol = (dp, 0) if up else (0, dp)

        def body(lr, rr):
            i = pl.program_id(0)
            for at_i, hook in hooks.items():
                at_step(i == at_i, hook)
            dw_step(kind, acc, lr, rr)

        pltpu.emit_pipeline(
            body,
            grid=(blocks,),
            in_specs=[
                pl.BlockSpec((BM, lw), lambda i: (row_block(i), lcol)),
                pl.BlockSpec((BM, rw), lambda i: (row_block(i), rcol)),
            ],
        )(lhs, rhs)

    def all_rows(i):
        return i

    def k_blocks(k):
        return lambda i: i * 4 + k

    def go(*copies):
        for cp in copies:
            cp.start()

    def pass_on(sh, s):
        sh["y"](s).wait_recv()
        go(sh["x"](s), sh["c"](s))

    def pass_core(sh, s):
        sh["x"](s).wait_recv()
        go(sh["f"](s))

    def pass_k(k):
        for d in (kx, kg):
            d(k).wait_recv()
        go(fkx(k), fkg(k))

    def have_k(k):
        for d in (fkx, fkg):
            d(k).wait_recv()

    def have(s):
        for sh in (sx0, sg1):
            for kind in "cf":
                sh[kind](s).wait_recv()

    def early(i):
        return lax.div(i, 2) * 4 + lax.rem(i, 2)

    def late(i):
        return lax.div(i, 2) * 4 + 2 + lax.rem(i, 2)

    go(kx(0), kg(0))
    load(1, "down").wait()
    run_own(1, gtop, {4: lambda: go(kx(1), kg(1))})
    pass_k(0)
    add_quarter(1, gtop, g1, 0)
    go(ag[1]["x"](0))

    def block1_own(acc):
        weights("down", acc, 0, aa.at[1], gtop, 8, all_rows, True)
        move(acc, 0, down1, True)
        add_quarter(1, gtop, g1, 1)
        go(ag[1]["x"](1), sx0["y"](0), sg1["y"](0))
        weights("up", acc, 0, x1, dh.at[1], 8, all_rows, True)
        move(acc, 0, up1, True)
        go(sx0["y"](1), sg1["y"](1))
        settle(0)

    pl.run_scoped(block1_own, pltpu.VMEM((2, NB, NB), F32))
    have_k(0)

    def on_k1():
        ag[1]["x"](0).wait_recv()
        go(ag[1]["f"](0))
        pass_k(1)

    peer(1, xp1, gp2, 2, k_blocks(0), {1: on_k1})
    have_k(1)
    peer(1, xp1, gp2, 2, k_blocks(1))
    go(load(0, "down"), load(0, "up"))
    ag[1]["x"](1).wait_recv()
    go(ag[1]["f"](1))
    for s in range(2):
        ag[1]["c"](s).wait_recv()
    ag[1]["f"](0).wait_recv()
    pass_on(sx0, 0)
    load(0, "down").wait()

    def own0_late():
        pass_core(sx0, 0)
        go(r2_copy(0, 0))

    run_own(0, g1, {4: lambda: pass_on(sg1, 0), 6: own0_late})
    go(kx(2), kg(2))

    def with_acc(fn):
        pl.run_scoped(fn, pltpu.VMEM((2, NB, NB), F32))

    def down_own(acc):
        weights("down", acc, 0, aa.at[0], g1, 8, all_rows, True,
                {1: lambda: pass_on(sx0, 1), 5: lambda: pass_core(sg1, 0)})
        move(acc, 0, down0, True)
        settle(0)

    def on_s1():
        pass_on(sg1, 1)
        go(r2_copy(0, 1), kx(3), kg(3))

    def up_own(acc):
        weights("up", acc, 0, x0, dh.at[0], 8, all_rows, True, {6: lambda: pass_core(sx0, 1)})
        move(acc, 0, up0, True)
        move(acc, 0, down1, False)
        weights("down", acc, 0, ap.at[1], gp2, 4, early)
        move(acc, 0, down1, True)
        settle(0)

    def down_late(acc):
        move(acc, 0, down1, False)
        weights("down", acc, 0, ap.at[1], gp2, 4, late)
        move(acc, 0, down1, True)
        ag[0]["x"](1).wait_recv()
        go(ag[0]["f"](1))
        settle(0)

    with_acc(down_own)
    have(0)
    peer(0, xp0, gp1, 4, lambda i: i * 2, {2: on_s1})
    add_quarter(0, g1, g0, 0)
    go(ag[0]["x"](0))
    with_acc(up_own)
    pass_core(sg1, 1)
    have(1)
    peer(0, xp0, gp1, 4, lambda i: i * 2 + 1, {2: lambda: pass_k(2)})
    go(load(1, "up"), load(1, "down"))
    add_quarter(0, g1, g0, 1)
    go(ag[0]["x"](1))
    have_k(2)
    load(1, "up").wait()
    load(1, "down").wait()
    peer(1, xp1, gp2, 2, k_blocks(2), {1: lambda: pass_k(3)})
    have_k(3)
    peer(1, xp1, gp2, 2, k_blocks(3))
    ag[0]["x"](0).wait_recv()
    go(ag[0]["f"](0))
    with_acc(down_late)
    for s in range(2):
        ag[0]["c"](s).wait_recv()
        ag[0]["f"](s).wait_recv()

    for k in range(4):
        for d in (kx, kg, fkx, fkg):
            d(k).wait_send()
    for l in range(2):
        for s in range(2):
            r2_copy(l, s).wait_send()
            for kind in "xcf":
                ag[l][kind](s).wait_send()
    for sh in (sx0, sg1):
        for kind in "yxcf":
            for s in range(2):
                sh[kind](s).wait_send()


N_COPIES = 72


def finish_kernel(
    xp0, gp1, xp1, gp2, dhp, ap, down0, up0, down1, up1, g0_in,
    g0, dw_up, dw_down,
    acc_d, acc_u, acc_l, mbuf, gbuf, sem, msem, ssem, bsem,
):
    dp = lax.axis_index("dp")
    tokens, width = g0_in.shape
    NB = width // 2
    blocks = tokens // BM

    def acc_in(acc, src, which):
        return [pltpu.make_async_copy(src.at[i], acc.at[i], sem.at[which * 2 + i]) for i in range(2)]

    def acc_out(kind, acc, dst, which):
        return [pltpu.make_async_copy(acc.at[i], halves(kind, dst, i, NB), sem.at[which * 2 + i]) for i in range(2)]

    def start(copies):
        for cp in copies:
            cp.start()

    def wait(copies):
        for cp in copies:
            cp.wait()

    piece = NB // 8

    def strip_in(acc, src, p, sem):
        h, r = lax.div(p, 8), pl.multiple_of(lax.rem(p, 8) * piece, piece)
        return pltpu.make_async_copy(src.at[h, pl.ds(r, piece)], acc.at[h, pl.ds(r, piece)], sem)

    def strip_out(kind, acc, dst, p, sem):
        h, r = lax.div(p, 8), pl.multiple_of(lax.rem(p, 8) * piece, piece)
        if kind == "up":
            far = dst.at[pl.ds(r, piece), pl.ds(pl.multiple_of(h * NB, NB), NB)]
        else:
            far = dst.at[pl.ds(pl.multiple_of(p * piece, piece), piece)]
        return pltpu.make_async_copy(acc.at[h, pl.ds(r, piece)], far, sem)

    def phase(kind, acc, lhs, rhs, steps, row_block, g_first, moves_m, ins, outs):
        lw, rw = (NB, width) if kind == "up" else (width, NB)
        lcol, rcol = (dp, 0) if kind == "up" else (0, dp)
        per = 16 // steps
        gb = tokens // 16

        def g_move(i, out_side):
            slot = lax.rem(i, 2)
            rows = pl.ds(pl.multiple_of((g_first + i) * gb, gb), gb)
            if out_side:
                return pltpu.make_async_copy(gbuf.at[slot], g0.at[0, rows], msem.at[1, slot])
            return pltpu.make_async_copy(g0_in.at[rows], gbuf.at[slot], msem.at[0, slot])

        def m_move(p, out_side):
            slot = lax.rem(p, 4)
            h, r = lax.div(p, 8), pl.multiple_of(lax.rem(p, 8) * piece, piece)
            if out_side:
                far = dw_down.at[1, pl.ds(pl.multiple_of(p * piece, piece), piece)]
                return pltpu.make_async_copy(mbuf.at[slot], far, bsem.at[1, slot])
            return pltpu.make_async_copy(down1.at[h, pl.ds(r, piece)], mbuf.at[slot], bsem.at[0, slot])

        def m_pair(i):
            return [i * 2, i * 2 + 1] if moves_m else []

        def strips(i):
            res = []
            for k in range(per):
                for args in ins:
                    res.append(strip_in(*args, i * per + k, ssem.at[len(res)]))
                for args in outs:
                    res.append(strip_out(*args, i * per + k, ssem.at[len(res)]))
            return res

        moves_g = g_first is not None
        if moves_g:
            g_move(0, False).start()
        start([m_move(p, False) for p in m_pair(0)])

        def body(lr, rr):
            i = pl.program_id(0)

            @pl.when(i > 0)
            def _():
                wait(strips(i - 1))

            start(strips(i))
            wait([m_move(p, False) for p in m_pair(i)])
            start([m_move(p, True) for p in m_pair(i)])
            if moves_m:
                @pl.when(i > 0)
                def _():
                    wait([m_move(p, True) for p in m_pair(i - 1)])

                @pl.when(i < steps - 1)
                def _():
                    start([m_move(p, False) for p in m_pair(i + 1)])
            if moves_g:
                g_move(i, False).wait()
                g_move(i, True).start()

                @pl.when(i > 0)
                def _():
                    g_move(i - 1, True).wait()

                @pl.when(i < steps - 1)
                def _():
                    g_move(i + 1, False).start()

            dw_step(kind, acc, lr, rr)

        pltpu.emit_pipeline(
            body, grid=(steps,),
            in_specs=[
                pl.BlockSpec((BM, lw), lambda i: (row_block(i), lcol)),
                pl.BlockSpec((BM, rw), lambda i: (row_block(i), rcol)),
            ],
        )(lhs, rhs)
        wait(strips(steps - 1))
        wait([m_move(p, True) for p in m_pair(steps - 1)])
        if moves_g:
            g_move(steps - 1, True).wait()

    every = lambda i: i
    start(acc_in(acc_d, down0, 0))
    wait(acc_in(acc_d, down0, 0))
    phase("down", acc_d, ap.at[0], gp1, blocks, every, 0, True, [(acc_u, up0)], [])
    phase("up", acc_u, xp0, dhp.at[0], blocks, every, blocks, False, [(acc_l, up1)], [("down", acc_d, dw_down.at[0])])
    phase("up", acc_l, xp1, dhp.at[1], blocks, every, None, False, [], [("up", acc_u, dw_up.at[0])])
    start(acc_out("up", acc_l, dw_up.at[1], 1))
    wait(acc_out("up", acc_l, dw_up.at[1], 1))


def solution(mesh):
    def local_backward(w_up, w_down, saved_x, saved_h, grad_out):
        tokens, width = grad_out.shape[1:]
        row = jax.ShapeDtypeStruct((tokens, width), BF16)
        two = jax.ShapeDtypeStruct((2, tokens, width), BF16)
        quarter = jax.ShapeDtypeStruct((2, tokens // 4, width), BF16)
        sums = jax.ShapeDtypeStruct((2, width // 2, width // 2), F32)
        outs = [row, row, two, two, two, quarter, row, row, row, row, two, two, sums, sums, sums, sums]
        flops = 2 * tokens * width * width
        g0, g1, dh, aa, ps, r2, xp1, gp2, xp0, gp1, dhp, ap, down1, up1, down0, up0 = pl.pallas_call(
            main_kernel,
            out_shape=outs,
            in_specs=[ANY] * 5,
            out_specs=[ANY] * len(outs),
            scratch_shapes=[
                pltpu.VMEM((width, width), BF16),
                pltpu.VMEM((width, width), BF16),
                pltpu.VMEM((2, 2, BM, width // 2), BF16),
                pltpu.SemaphoreType.DMA((2,)),
                pltpu.SemaphoreType.DMA((4,)),
                pltpu.SemaphoreType.DMA((2,)),
                pltpu.SemaphoreType.DMA((N_COPIES,)),
                pltpu.SemaphoreType.DMA((N_COPIES,)),
            ],
            compiler_params=pltpu.CompilerParams(
                collective_id=0, has_side_effects=True, vmem_limit_bytes=VMEM_LIMIT),
            cost_estimate=pl.CostEstimate(flops=11 * flops, bytes_accessed=10**9, transcendentals=0),
            name="backward_main",
        )(w_up, w_down, saved_x, saved_h, grad_out)
        return tuple(pl.pallas_call(
            finish_kernel,
            out_shape=[
                jax.ShapeDtypeStruct((1, tokens, width), BF16),
                jax.ShapeDtypeStruct((2, width // 2, width), F32),
                jax.ShapeDtypeStruct((2, width, width // 2), F32),
            ],
            in_specs=[ANY] * 11,
            out_specs=[ANY] * 3,
            scratch_shapes=[
                pltpu.VMEM(sums.shape, F32),
                pltpu.VMEM(sums.shape, F32),
                pltpu.VMEM(sums.shape, F32),
                pltpu.VMEM((4, width // 16, width // 2), F32),
                pltpu.VMEM((2, BM // 2, width), BF16),
                pltpu.SemaphoreType.DMA((4,)),
                pltpu.SemaphoreType.DMA((2, 2)),
                pltpu.SemaphoreType.DMA((8,)),
                pltpu.SemaphoreType.DMA((2, 4)),
            ],
            compiler_params=pltpu.CompilerParams(vmem_limit_bytes=VMEM_LIMIT),
            cost_estimate=pl.CostEstimate(flops=flops, bytes_accessed=3 * 10**8, transcendentals=0),
            name="backward_finish",
        )(xp0, gp1, xp1, gp2, dhp, ap, down0, up0, down1, up1, g0))

    return jax.shard_map(
        local_backward,
        mesh=mesh,
        in_specs=(P(None, None, "tp"), P(None, "tp", None), P(None, "dp", None, None), P(None, "dp", None, "tp"), P("dp", None, None)),
        out_specs=(P("dp", None, None), P(None, "dp", "tp"), P(None, "tp", "dp")),
        check_vma=False,
    )
```

time: 1040 us -> 892 us (0.86)
  Pallas kernels: 1030 us -> 880 us
    pallas_call x1, Pallas kernels: 944 us -> 772 us  [local_backward(): pl.pallas_call(main_kernel, out_shape=outs, in_specs=[ANY] * 5, out_specs...]
    pallas_call x1, Pallas kernels: 88.5 us -> 108 us  [local_backward(): pl.pallas_call(finish_kernel, out_shape=[jax.ShapeDtypeStruct((1, tokens,...]
where the time goes in v2:
time: 892 us; the launch traced here: 881 us
  Pallas kernels  880 us (99%)
    pallas_call x1, Pallas kernels, local_backward(): pl.pallas_call(main_kernel, out_shape=outs, in_specs=[ANY] * 5, out_specs...  772 us
    pallas_call x1, Pallas kernels, local_backward(): pl.pallas_call(finish_kernel, out_shape=[jax.ShapeDtypeStruct((1, tokens,...  108 us

profile of v2, /device:TPU:0, one launch (start us, length us, event | category | flops | bytes accessed | tf_op | source)
XLA Modules:
  0.0 881.1 jit_solution(640158099730065696)
XLA Ops:
  0.6 771.6 %backward_main.1 = (bf16[4096,2560]{1,0:T(8,128)(2,1)}, bf16[4096,2560]{1,0:T(8,128)(2,1)}, bf16[2,4096,2560]{2,1,0:T(8,128)(2,1)}, bf16[2,4096,2560]{2,1,0:T(8,...) custom-call(bf16[2,2560,2560]{2,1,0:T(8,128)(2,1)} %w_up.1, ...), custom_call_target="tpu_custom_call" | custom-call | flops 590558003200 | bytes 1000000000 | tf_op jit(solution)/shard_map/backward_main/pallas_call | solution.py:619
  772.2 108.5 %backward_finish.1 = (bf16[1,4096,2560]{2,1,0:T(8,128)(2,1)}, f32[2,1280,2560]{2,1,0:T(8,128)}, f32[2,2560,1280]{2,1,0:T(8,128)}) custom-call(bf16[4096,2560]{1,0:T(8,128)(2,1)} %get-tuple-element.14.xp0, bf16[4096,2560]{1,0:T(8,128)(2,1)} %get-tuple-element.15.gp1, bf16[4096,2560]{1,0:T(8,128)(2,1)} %get-tuple-element.16.xp1, ...), custom_call_target="tpu_custom_call" | custom-call | flops 53687091200 | bytes 300000000 | tf_op jit(solution)/shard_map/backward_finish/pallas_call | solution.py:639
